TPU v7x, 32 devices: a whole 2x2x4 slice. The times are simulated.
32 devices in a mesh: lat: 4 (over z), lon: 4 (over y, x), obs: 2 (over core).
Axes of the slice: x: 2, y: 2, z: 4, core: 2. Of those that a mesh axis runs over, the one named last changes fastest.
Arguments:
- innovation: float32 [4096, 128], P(('lat', 'lon', 'obs')), may hold values from -6 to 6
- obs_error: float32 [4096, 128], P(('lat', 'lon', 'obs')), may hold values from 0.5 to 2
- obs_offset: float32 [2, 4096, 128], P(None, ('lat', 'lon', 'obs')), may hold values from 0 to 1
- obs_cell: int32 [4096, 128], P(('lat', 'lon', 'obs')), may hold values from 0 to 65535
- obs_owner: int32 [32, 128], P(('lat', 'lon', 'obs')), may hold values from 0 to 15, as said below
- block_count: int32 [32], P(('lat', 'lon', 'obs')), may hold values from 64 to 128
- land_mask: int32 [256, 4096], P(('lat', 'obs'), 'lon'), may hold values from 0 to 1, as said below
- inertia: float32 [256, 4096], P(('lat', 'obs'), 'lon'), may hold values from 0.002 to 0.05
- sea_depth: float32 [256, 4096], P(('lat', 'obs'), 'lon'), may hold values from 0.5 to 5
Outputs:
- adjoint_field: float32 [256, 4096], P(('lat', 'obs'), 'lon')
- residual: float32 [256, 4096], P(('lat', 'obs'), 'lon')
Inputs may be any that keep to these rules, and one draw needn't show every extreme that they name: `obs_owner`: among the live blocks of one device at most 16 name the same tile; in every draw some tile is named by exactly 16 live blocks of every device. `land_mask`: the first and the last grid row are land.
All inputs are finite; a program needn't handle non-finite values.
Results may differ from a plain program's by a relative error of at most 0.0003.
Values sent between devices are 32-bit elements; how exact they have to be, the bound alone decides.
A program may use at most 64 MiB of HBM per device.

v0:
```python
import jax
import jax.numpy as jnp
from jax import lax
from jax.sharding import PartitionSpec as P

ITERS = 5


def extended(block, sides, width):
    for axis, dim in sides:
        count = lax.axis_size(axis)
        forward = [(i, i + 1) for i in range(count - 1)]
        forward.append((count - 1, 0))
        backward = [(target, source) for source, target in forward]
        low = lax.ppermute(
            lax.slice_in_dim(block, block.shape[dim] - width, None, axis=dim), axis, forward
        )
        high = lax.ppermute(lax.slice_in_dim(block, 0, width, axis=dim), axis, backward)
        block = jnp.concatenate([low, block, high], axis=dim)
    return block


def shifted(value, axis, steps):
    count = lax.axis_size(axis)
    pairs = [(source, (source + steps) % count) for source in range(count)]
    return lax.ppermute(value, axis, pairs)


def shifted_2(block, axis, distance):
    devices = range(lax.axis_size(axis))
    route = [(i - distance, i) for i in devices if i - distance in devices]
    return lax.ppermute(block, axis, route)


def border(field):
    return extended(field, ((("lat", "obs"), 0), ("lon", 1)), 1)


def two_products(residual, applied):
    return lax.psum(
        (jnp.sum(residual * residual), jnp.sum(residual * applied)), ("lat", "lon", "obs")
    )


def body(
    innovation,
    obs_error,
    obs_offset,
    obs_cell,
    obs_owner,
    block_count,
    land_mask,
    inertia,
    sea_depth,
):
    block_total = obs_owner.shape[1]
    block_width = innovation.shape[1]
    n_lat = lax.axis_size("lat")
    n_lon = lax.axis_size("lon")
    tile_count = n_lat * n_lon
    capacity = max(3, 2 * ((block_total + tile_count - 1) // tile_count))
    slot_total = tile_count * capacity
    tile_rows = land_mask.shape[0] * lax.axis_size("obs")
    tile_cols = land_mask.shape[1]
    owners = obs_owner[0]
    block_ids = jnp.arange(block_total)
    is_live = block_ids < block_count[0]
    earlier = block_ids[None, :] < block_ids[:, None]
    same_owner = (owners[None, :] == owners[:, None]) & earlier & is_live[None, :]
    slot_rank = jnp.sum(same_owner.astype(jnp.int32), axis=1)
    target = jnp.where(is_live, owners * capacity + slot_rank, slot_total)
    scaled = innovation / (obs_error * obs_error)
    floats = jnp.stack([scaled, obs_offset[0], obs_offset[1]], axis=1)

    def put_slots(values):
        holder = jnp.zeros((slot_total + 1,) + values.shape[1:], values.dtype)
        return holder.at[target].set(values)[:slot_total]

    sent_floats = put_slots(floats)
    sent_cells = put_slots(obs_cell)
    received, cell_ids = (
        lax.all_to_all(
            sent_floats.reshape(tile_count, capacity, 3, block_width),
            ("lat", "lon"),
            split_axis=0,
            concat_axis=0,
            tiled=True,
        ),
        lax.all_to_all(
            sent_cells.reshape(tile_count, capacity, block_width),
            ("lat", "lon"),
            split_axis=0,
            concat_axis=0,
            tiled=True,
        ),
    )
    received = received.reshape(-1, 3, block_width)
    cell_ids = cell_ids.reshape(-1, block_width)
    group = 1
    for size_try in range(1, slot_total + 1):
        if slot_total % size_try == 0 and size_try * block_width <= 4096:
            group = size_try
    turns = slot_total // group
    group_obs = group * block_width
    scaled_in = received[:, 0].reshape(turns, group_obs)
    north_frac = received[:, 1].reshape(turns, group_obs)
    east_frac = received[:, 2].reshape(turns, group_obs)
    cells_in = cell_ids.reshape(turns, group_obs)
    wide = tile_cols + 1
    row_axis = jnp.arange(tile_rows + 1, dtype=jnp.int32)[:, None]
    col_axis = jnp.arange(wide, dtype=jnp.int32)[None, :]

    def spread(total, pieces):
        amount, north, east, cells = pieces
        cell_row = (cells // tile_cols)[None, :]
        cell_col = (cells % tile_cols)[:, None]
        row_weights = (
            jnp.where(row_axis == cell_row, 1.0 - north[None, :], 0.0)
            + jnp.where(row_axis == cell_row + 1, north[None, :], 0.0)
        ) * amount[None, :]
        col_weights = jnp.where(col_axis == cell_col, 1.0 - east[:, None], 0.0) + jnp.where(
            col_axis == cell_col + 1, east[:, None], 0.0
        )
        return (
            total
            + jnp.dot(
                row_weights,
                col_weights,
                precision=lax.Precision.HIGHEST,
                preferred_element_type=jnp.float32,
            ),
            None,
        )

    partial_value, unused = lax.scan(
        spread,
        jnp.zeros((tile_rows + 1, wide), jnp.float32),
        (scaled_in, north_frac, east_frac, cells_in),
    )
    arrived_col = shifted(partial_value[:, tile_cols], "lon", 1)
    partial_value = partial_value[:, :tile_cols].at[:, 0].add(arrived_col)
    arrived_row = shifted_2(partial_value[tile_rows], "lat", 1)
    tile_part = partial_value[:tile_rows].at[0].add(arrived_row)
    ocean = land_mask.astype(jnp.float32)
    forcing = lax.psum_scatter(tile_part, "obs", scatter_dimension=0, tiled=True) * ocean
    conduct = ocean * sea_depth
    padded = border(conduct)
    cond_north = jnp.sqrt(conduct * padded[:-2, 1:-1])
    cond_south = jnp.sqrt(conduct * padded[2:, 1:-1])
    cond_west = jnp.sqrt(conduct * padded[1:-1, :-2])
    cond_east = jnp.sqrt(conduct * padded[1:-1, 2:])
    diagonal = inertia + cond_north + cond_south + cond_west + cond_east

    def operate(field):
        outer = border(field)
        return (
            diagonal * field
            - cond_north * outer[:-2, 1:-1]
            - cond_south * outer[2:, 1:-1]
            - cond_west * outer[1:-1, :-2]
            - cond_east * outer[1:-1, 2:]
        )

    adjoint_field = jnp.zeros_like(forcing)
    residual = forcing
    applied = operate(residual)
    norm_now, product = two_products(residual, applied)
    step_size = norm_now / product
    direction = residual
    applied_dir = applied
    for iteration in range(ITERS):
        adjoint_field = adjoint_field + step_size * direction
        residual = residual - step_size * applied_dir
        if iteration + 1 < ITERS:
            applied = operate(residual)
            norm_next, product = two_products(residual, applied)
            beta_ratio = norm_next / norm_now
            step_size = norm_next / (product - beta_ratio * norm_next / step_size)
            direction = residual + beta_ratio * direction
            applied_dir = applied + beta_ratio * applied_dir
            norm_now = norm_next
    return (adjoint_field, residual)


def solution(mesh):
    in_specs = (
        P(("lat", "lon", "obs"), None),
        P(("lat", "lon", "obs"), None),
        P(None, ("lat", "lon", "obs"), None),
        P(("lat", "lon", "obs"), None),
        P(("lat", "lon", "obs"), None),
        P(("lat", "lon", "obs")),
        P(("lat", "obs"), "lon"),
        P(("lat", "obs"), "lon"),
        P(("lat", "obs"), "lon"),
    )
    out_specs = (P(("lat", "obs"), "lon"), P(("lat", "obs"), "lon"))
    return jax.shard_map(body, mesh=mesh, in_specs=in_specs, out_specs=out_specs, check_vma=False)
```

profile of v0, /device:TPU:14, one launch (start us, length us, event | category | flops | bytes accessed | tf_op | source)
XLA Modules:
  0.0 499.8 jit_solution(3898041280866517940)
XLA Ops:
  11.3 7.1 %all-to-all-start = ((s32[16,16,128]{2,1,0:T(8,128)}), s32[16,16,128]{2,1,0:T(8,128)S(1)}, u32[]{:S(2)}, u32[]{:S(2)}) async-start(s32[16,16,128]{2,1,0:T(8,128)} %bitcast.5), calls=%async_computation | async-start | bytes 262144 | tf_op jit(solution)/shard_map/all_to_all | solution.py:89
  18.8 4.4 scatter_fusion
  24.0 7.0 %all-to-all-start.1 = ((f32[16,16,3,128]{3,1,2,0:T(8,128)}), f32[16,16,3,128]{3,1,2,0:T(8,128)S(1)}, u32[]{:S(2)}, u32[]{:S(2)}) async-start(f32[16,16,3,128]{3,1,2,0:T(8,128)} %copy.29), calls=%async_computation.1 | async-start | bytes 786432 | tf_op jit(solution)/shard_map/all_to_all | solution.py:82
  31.1 9.6 %all-to-all-done.1 = f32[16,16,3,128]{3,1,2,0:T(8,128)S(1)} async-done(((f32[16,16,3,128]{3,1,2,0:T(8,128)}), f32[16,16,3,128]{3,1,2,0:T(8,128)S(1)}, u32[]{:S(2)}, u32[]{:S(2)}) %all-to-all-start.1) | async-done | bytes 393248 | tf_op jit(solution)/shard_map/all_to_all | solution.py:82
  40.9 152.0 %while.16 = (s32[]{:T(128)}, f32[65,1025]{1,0:T(8,128)S(1)}, s32[8,4096]{1,0:T(8,128)S(1)}, f32[8,4096]{1,0:T(8,128)S(1)}, f32[8,4096]{1,0:T(8,128)S(1)}, /*index=5*/f32[8,4096]{1,0:T(8,128)S(1)}, s32[]{:T(128)}, s32[]{:T(128)}) while((s32[]{:T(128)}, f32[65,1025]{1,0:T(8,128)S(1)}, s32[8,4096]{1,0:T(8,128)S(1)}, ...), condition=%wide.region_4.5_spmd.clone.clone, body=%wide.region_3.4_spmd.clone.clone.sunk | while | flops 3297597440 | bytes 942707 | solution.py:135
  41.1 18.7 %fusion.98 = f32[65,1025]{1,0:T(8,128)S(1)} fusion(f32[4096]{0:T(1024)S(1)} %bitcast.58, s32[4096]{0:T(1024)S(1)} %get-tuple-element.312, f32[4096]{0:T(1024)S(1)} %broadcast_subtract_fusion.5, s32[4096]{0:T(1024)S(1)} %get-tuple-element.313, f32[4096]{0:T(1024)S(1)} %bitcast.63, f32[4096]{0:T(1024)S(1)} %bitcast.62, s32[4096]{0:T(1024)S(1)} %bitcast.64, ...), kind=kOutput, calls=%fused_computation.15.clone.1 | convolution fusion | flops 3297474560 | bytes 680457 | tf_op jit(solution)/shard_map/while/body/eval_jaxpr/dot_general | solution.py:126
  60.1 18.7 %fusion.98 = f32[65,1025]{1,0:T(8,128)S(1)} fusion(f32[4096]{0:T(1024)S(1)} %bitcast.58, s32[4096]{0:T(1024)S(1)} %get-tuple-element.312, f32[4096]{0:T(1024)S(1)} %broadcast_subtract_fusion.5, s32[4096]{0:T(1024)S(1)} %get-tuple-element.313, f32[4096]{0:T(1024)S(1)} %bitcast.63, f32[4096]{0:T(1024)S(1)} %bitcast.62, s32[4096]{0:T(1024)S(1)} %bitcast.64, ...), kind=kOutput, calls=%fused_computation.15.clone.1 | convolution fusion | flops 3297474560 | bytes 680457 | tf_op jit(solution)/shard_map/while/body/eval_jaxpr/dot_general | solution.py:126
  79.1 18.7 %fusion.98 = f32[65,1025]{1,0:T(8,128)S(1)} fusion(f32[4096]{0:T(1024)S(1)} %bitcast.58, s32[4096]{0:T(1024)S(1)} %get-tuple-element.312, f32[4096]{0:T(1024)S(1)} %broadcast_subtract_fusion.5, s32[4096]{0:T(1024)S(1)} %get-tuple-element.313, f32[4096]{0:T(1024)S(1)} %bitcast.63, f32[4096]{0:T(1024)S(1)} %bitcast.62, s32[4096]{0:T(1024)S(1)} %bitcast.64, ...), kind=kOutput, calls=%fused_computation.15.clone.1 | convolution fusion | flops 3297474560 | bytes 680457 | tf_op jit(solution)/shard_map/while/body/eval_jaxpr/dot_general | solution.py:126
  98.1 18.7 %fusion.98 = f32[65,1025]{1,0:T(8,128)S(1)} fusion(f32[4096]{0:T(1024)S(1)} %bitcast.58, s32[4096]{0:T(1024)S(1)} %get-tuple-element.312, f32[4096]{0:T(1024)S(1)} %broadcast_subtract_fusion.5, s32[4096]{0:T(1024)S(1)} %get-tuple-element.313, f32[4096]{0:T(1024)S(1)} %bitcast.63, f32[4096]{0:T(1024)S(1)} %bitcast.62, s32[4096]{0:T(1024)S(1)} %bitcast.64, ...), kind=kOutput, calls=%fused_computation.15.clone.1 | convolution fusion | flops 3297474560 | bytes 680457 | tf_op jit(solution)/shard_map/while/body/eval_jaxpr/dot_general | solution.py:126
  117.1 18.7 %fusion.98 = f32[65,1025]{1,0:T(8,128)S(1)} fusion(f32[4096]{0:T(1024)S(1)} %bitcast.58, s32[4096]{0:T(1024)S(1)} %get-tuple-element.312, f32[4096]{0:T(1024)S(1)} %broadcast_subtract_fusion.5, s32[4096]{0:T(1024)S(1)} %get-tuple-element.313, f32[4096]{0:T(1024)S(1)} %bitcast.63, f32[4096]{0:T(1024)S(1)} %bitcast.62, s32[4096]{0:T(1024)S(1)} %bitcast.64, ...), kind=kOutput, calls=%fused_computation.15.clone.1 | convolution fusion | flops 3297474560 | bytes 680457 | tf_op jit(solution)/shard_map/while/body/eval_jaxpr/dot_general | solution.py:126
  136.0 18.7 %fusion.98 = f32[65,1025]{1,0:T(8,128)S(1)} fusion(f32[4096]{0:T(1024)S(1)} %bitcast.58, s32[4096]{0:T(1024)S(1)} %get-tuple-element.312, f32[4096]{0:T(1024)S(1)} %broadcast_subtract_fusion.5, s32[4096]{0:T(1024)S(1)} %get-tuple-element.313, f32[4096]{0:T(1024)S(1)} %bitcast.63, f32[4096]{0:T(1024)S(1)} %bitcast.62, s32[4096]{0:T(1024)S(1)} %bitcast.64, ...), kind=kOutput, calls=%fused_computation.15.clone.1 | convolution fusion | flops 3297474560 | bytes 680457 | tf_op jit(solution)/shard_map/while/body/eval_jaxpr/dot_general | solution.py:126
  155.0 18.7 %fusion.98 = f32[65,1025]{1,0:T(8,128)S(1)} fusion(f32[4096]{0:T(1024)S(1)} %bitcast.58, s32[4096]{0:T(1024)S(1)} %get-tuple-element.312, f32[4096]{0:T(1024)S(1)} %broadcast_subtract_fusion.5, s32[4096]{0:T(1024)S(1)} %get-tuple-element.313, f32[4096]{0:T(1024)S(1)} %bitcast.63, f32[4096]{0:T(1024)S(1)} %bitcast.62, s32[4096]{0:T(1024)S(1)} %bitcast.64, ...), kind=kOutput, calls=%fused_computation.15.clone.1 | convolution fusion | flops 3297474560 | bytes 680457 | tf_op jit(solution)/shard_map/while/body/eval_jaxpr/dot_general | solution.py:126
  174.0 18.7 %fusion.98 = f32[65,1025]{1,0:T(8,128)S(1)} fusion(f32[4096]{0:T(1024)S(1)} %bitcast.58, s32[4096]{0:T(1024)S(1)} %get-tuple-element.312, f32[4096]{0:T(1024)S(1)} %broadcast_subtract_fusion.5, s32[4096]{0:T(1024)S(1)} %get-tuple-element.313, f32[4096]{0:T(1024)S(1)} %bitcast.63, f32[4096]{0:T(1024)S(1)} %bitcast.62, s32[4096]{0:T(1024)S(1)} %bitcast.64, ...), kind=kOutput, calls=%fused_computation.15.clone.1 | convolution fusion | flops 3297474560 | bytes 680457 | tf_op jit(solution)/shard_map/while/body/eval_jaxpr/dot_general | solution.py:126
  193.1 2.1 collective-permute-start
  197.6 1.9 collective-permute-start.1
  199.6 3.5 collective-permute-done.1
  204.0 8.9 %reduce-scatter.2.cloned.1.call-done = f32[32,1024]{1,0:T(8,128)} async-done(((f32[64,1024]{1,0:T(8,128)}), f32[32,1024]{1,0:T(8,128)}) %reduce-scatter.2.cloned.1.call-update) | async-done | bytes 131088 | tf_op jit(solution)/shard_map/reduce_scatter | solution.py:145
  215.7 1.7 collective-permute-start.7
  223.5 2.3 collective-permute-done.9
  226.7 44.0 %all-reduce.4 = (f32[]{:T(128)}, f32[]{:T(128)}) all-reduce(f32[]{:T(128)} %get-tuple-element.194, f32[]{:T(128)} %get-tuple-element.193), channel_id=1, replica_groups=mesh['lat'=4,'lon'=4,'obs'=2] {'lat','lon','obs'}, use_global_device_ids=true, to_apply=%region_8.9 | all-reduce | flops 2 | bytes 16 | tf_op jit(solution)/shard_map/psum | solution.py:40
  275.3 2.0 collective-permute-start.13
  277.3 1.8 collective-permute-done.12
  281.0 41.2 %all-reduce.3 = (f32[]{:T(128)}, f32[]{:T(128)}) all-reduce(f32[]{:T(128)} %get-tuple-element.192, f32[]{:T(128)} %get-tuple-element.191), channel_id=1, replica_groups=mesh['lat'=4,'lon'=4,'obs'=2] {'lat','lon','obs'}, use_global_device_ids=true, to_apply=%region_12.13 | all-reduce | flops 2 | bytes 16 | tf_op jit(solution)/shard_map/psum | solution.py:40
  329.9 2.0 collective-permute-start.17
  332.0 1.8 collective-permute-done.16
  335.6 42.7 %all-reduce.2 = (f32[]{:T(128)}, f32[]{:T(128)}) all-reduce(f32[]{:T(128)} %get-tuple-element.190, f32[]{:T(128)} %get-tuple-element.189), channel_id=1, replica_groups=mesh['lat'=4,'lon'=4,'obs'=2] {'lat','lon','obs'}, use_global_device_ids=true, to_apply=%region_16.17 | all-reduce | flops 2 | bytes 16 | tf_op jit(solution)/shard_map/psum | solution.py:40
  385.6 2.0 collective-permute-start.21
  387.6 1.8 collective-permute-done.20
  391.2 41.8 %all-reduce.1 = (f32[]{:T(128)}, f32[]{:T(128)}) all-reduce(f32[]{:T(128)} %get-tuple-element.188, f32[]{:T(128)} %get-tuple-element.187), channel_id=1, replica_groups=mesh['lat'=4,'lon'=4,'obs'=2] {'lat','lon','obs'}, use_global_device_ids=true, to_apply=%region_20.21 | all-reduce | flops 2 | bytes 16 | tf_op jit(solution)/shard_map/psum | solution.py:40
  440.2 2.0 collective-permute-start.25
  442.2 1.8 collective-permute-done.24
  445.8 42.4 %all-reduce = (f32[]{:T(128)}, f32[]{:T(128)}) all-reduce(f32[]{:T(128)} %get-tuple-element.186, f32[]{:T(128)} %get-tuple-element.185), channel_id=1, replica_groups=mesh['lat'=4,'lon'=4,'obs'=2] {'lat','lon','obs'}, use_global_device_ids=true, to_apply=%region_24.25 | all-reduce | flops 2 | bytes 16 | tf_op jit(solution)/shard_map/psum | solution.py:40
  (149 shorter events, 40.6 us)
Async XLA Ops:
  11.3 12.7 %all-to-all-start = ((s32[16,16,128]{2,1,0:T(8,128)}), s32[16,16,128]{2,1,0:T(8,128)S(1)}, u32[]{:S(2)}, u32[]{:S(2)}) async-start(s32[16,16,128]{2,1,0:T(8,128)} %bitcast.5), calls=%async_computation | async-start | bytes 262144 | tf_op jit(solution)/shard_map/all_to_all | solution.py:89
  24.0 16.7 %all-to-all-start.1 = ((f32[16,16,3,128]{3,1,2,0:T(8,128)}), f32[16,16,3,128]{3,1,2,0:T(8,128)S(1)}, u32[]{:S(2)}, u32[]{:S(2)}) async-start(f32[16,16,3,128]{3,1,2,0:T(8,128)} %copy.29), calls=%async_computation.1 | async-start | bytes 786432 | tf_op jit(solution)/shard_map/all_to_all | solution.py:82
  31.1 181.8 %reduce-scatter.2.cloned.1.call-start = ((), (), s32[]{:S(2)}) async-start(), calls=%async_computation.3 | async-start | bytes 393216 | tf_op jit(solution)/shard_map/reduce_scatter | solution.py:145
  193.1 3.6 collective-permute-start
  196.1 16.8 %copy-start.2 = (f32[32,1024]{1,0:T(8,128)S(1)}, f32[32,1024]{1,0:T(8,128)}, u32[]{:S(2)}) copy-start(f32[32,1024]{1,0:T(8,128)} %param.23) | copy-start | bytes 393220
  196.1 16.8 %copy-start.3 = (s32[32,1024]{1,0:T(8,128)S(1)}, s32[32,1024]{1,0:T(8,128)}, u32[]{:S(2)}) copy-start(s32[32,1024]{1,0:T(8,128)} %param.21) | copy-start | bytes 393220
  197.6 5.5 %collective-permute-start.1 = (f32[1024]{0:T(1024)S(1)}, f32[1024]{0:T(1024)S(1)}, u32[]{:S(2)}, u32[]{:S(2)}) collective-permute-start(f32[1024]{0:T(1024)S(1)} %bitcast.68), channel_id=1, source_target_pairs={{0,8},{8,16},{16,24},{1,9},{9,17},{17,25},{2,10},{10,18},{18,26},{... | collective-permute-start | bytes 12296 | tf_op jit(solution)/shard_map/ppermute | solution.py:32
  204.0 21.8 %copy-start = (f32[32,1024]{1,0:T(8,128)S(1)}, f32[32,1024]{1,0:T(8,128)}, u32[]{:S(2)}) copy-start(f32[32,1024]{1,0:T(8,128)} %param.22) | copy-start | bytes 393220
  213.8 3.6 collective-permute-start.2
  214.2 3.2 collective-permute-start.3
  215.6 3.9 collective-permute-start.6
  215.7 3.9 collective-permute-start.7
  217.5 4.1 collective-permute-start.4
  218.1 4.8 collective-permute-start.5
  219.6 3.9 collective-permute-start.8
  221.1 4.7 collective-permute-start.9
  272.0 3.1 collective-permute-start.10
  272.1 3.1 collective-permute-start.11
  275.2 3.8 collective-permute-start.12
  275.3 4.7 collective-permute-start.13
  326.7 3.1 collective-permute-start.14
  326.8 3.1 collective-permute-start.15
  329.9 3.8 collective-permute-start.16
  329.9 4.7 collective-permute-start.17
  382.3 3.1 collective-permute-start.18
  382.4 3.1 collective-permute-start.19
  385.5 3.8 collective-permute-start.20
  385.6 4.7 collective-permute-start.21
  437.0 3.1 collective-permute-start.22
  437.0 3.1 collective-permute-start.23
  440.2 3.8 collective-permute-start.24
  440.2 4.7 collective-permute-start.25
  (4 other events, 34.7 us)
Sparse Core Ops, SparseCore 0:
  204.1 8.7 reduce-scatter.1
where the time goes:
time: 501 us; the launch traced here: 500 us
  blocking collectives  212 us (42%)
  matrix products  150 us (30%)
  waiting for transfers between devices  42.9 us (9%)
  starting transfers between devices  41.1 us (8%)
  between operations  32.8 us (7%)
  other arithmetic  11.1 us (2%)
  local copies, waits for them, and re-layouts  9.14 us (2%)
    psum x5, blocking collectives, two_products(): lax.psum((jnp.sum(residual * residual), jnp.sum(residual * applied)), ('l...  212 us
    dot_general x8, matrix products, spread(): jnp.dot(row_weights, col_weights, precision=lax.Precision.HIGHEST, prefer...  150 us
    ppermute x12, starting transfers between devices, extended(): lax.ppermute(lax.slice_in_dim(block, 0, width, axis=dim), axis, backward)  20.2 us
    ppermute x12, waiting for transfers between devices, extended(): lax.ppermute(lax.slice_in_dim(block, block.shape[dim] - width, None, axis...  12.8 us
  transfers between devices with their start and end apart: 29, of which 19 were waited for; matrix products, arithmetic and copies ran while one was open for 1% of the time, Pallas kernels for 0%

commit v1 on v0

--- a/solution.py
+++ b/solution.py
@@ -4,6 +4,11 @@
 from jax.sharding import PartitionSpec as P
 
 ITERS = 5
+
+
+def one_after_other(x, first, second):
+    inner = lax.psum(x, first)
+    return lax.psum(inner, second)
 
 
 def extended(block, sides, width):
@@ -37,8 +42,8 @@
 
 
 def two_products(residual, applied):
-    return lax.psum(
-        (jnp.sum(residual * residual), jnp.sum(residual * applied)), ("lat", "lon", "obs")
+    return one_after_other(
+        (jnp.sum(residual * residual), jnp.sum(residual * applied)), ("lon", "obs"), "lat"
     )
 
 

time: 501 us -> 431 us (0.86); the launches traced: 500 us -> 422 us
  blocking collectives: 212 us -> 123 us
  waiting for transfers between devices: 42.9 us -> 50.1 us
    psum x5 -> x10, blocking collectives: 212 us -> 123 us  [the longest x5 62.7 us: one_after_other(): return lax.psum(inner, second)]
    ppermute x12, starting transfers between devices: 2.7 us -> 13.8 us  [extended(): lax.ppermute(lax.slice_in_dim(block, block.shape[dim] - width, None, axis...]
    ppermute x12, waiting for transfers between devices: 7.43 us -> 15 us  [extended(): lax.ppermute(lax.slice_in_dim(block, 0, width, axis=dim), axis, backward)]
    ppermute x12, starting transfers between devices: 20.2 us -> 12.9 us  [extended(): lax.ppermute(lax.slice_in_dim(block, 0, width, axis=dim), axis, backward)]
  transfers between devices with their start and end apart: 29 -> 29, of which waited for: 19 -> 19; matrix products, arithmetic and copies ran while one was open for 1% -> 2% of each run, Pallas kernels for 0% -> 0%
where the time goes in v1:
time: 431 us; the launch traced here: 422 us
  matrix products  150 us (35%)
  blocking collectives  123 us (29%)
  waiting for transfers between devices  50.1 us (12%)
  starting transfers between devices  44.9 us (10%)
  between operations  32.8 us (8%)
  other arithmetic  11.1 us (3%)
  local copies, waits for them, and re-layouts  9.1 us (2%)
    dot_general x8, matrix products, spread(): jnp.dot(row_weights, col_weights, precision=lax.Precision.HIGHEST, prefer...  150 us
    psum x5, blocking collectives, one_after_other(): return lax.psum(inner, second)  62.7 us
    psum x5, blocking collectives, one_after_other(): inner = lax.psum(x, first)  60.7 us
    ppermute x12, waiting for transfers between devices, extended(): lax.ppermute(lax.slice_in_dim(block, 0, width, axis=dim), axis, backward)  15 us
    ppermute x12, starting transfers between devices, extended(): lax.ppermute(lax.slice_in_dim(block, block.shape[dim] - width, None, axis...  13.8 us
    ppermute x12, starting transfers between devices, extended(): lax.ppermute(lax.slice_in_dim(block, 0, width, axis=dim), axis, backward)  12.9 us
    ppermute x12, waiting for transfers between devices, extended(): lax.ppermute(lax.slice_in_dim(block, block.shape[dim] - width, None, axis...  12.4 us
    all_to_all x1, waiting for transfers between devices, body(): lax.all_to_all(sent_floats.reshape(tile_count, capacity, 3, block_width),...  9.6 us
  transfers between devices with their start and end apart: 29, of which 19 were waited for; matrix products, arithmetic and copies ran while one was open for 2% of the time, Pallas kernels for 0%

profile of v1, /device:TPU:14, one launch (start us, length us, event | category | flops | bytes accessed | tf_op | source)
XLA Modules:
  0.0 422.3 jit_solution(7166894645817641881)
XLA Ops:
  11.3 7.1 %all-to-all-start = ((s32[16,16,128]{2,1,0:T(8,128)}), s32[16,16,128]{2,1,0:T(8,128)S(1)}, u32[]{:S(2)}, u32[]{:S(2)}) async-start(s32[16,16,128]{2,1,0:T(8,128)} %bitcast.5), calls=%async_computation | async-start | bytes 262144 | tf_op jit(solution)/shard_map/all_to_all | solution.py:94
  18.8 4.4 %scatter_fusion = f32[257,3,128]{2,1,0:T(4,128)S(1)} fusion(f32[257,3,128]{2,1,0:T(4,128)S(1)} %broadcast_in_dim.100, s32[128]{0:T(128)S(1)} %fusion.80, f32[128,3,128]{2,1,0:T(4,128)S(1)} %copy.28), kind=kCustom, calls=%fused_computation.1 | custom fusion | bytes 590336 | tf_op jit(solution)/shard_map/scatter | solution.py:82
  24.0 7.0 %all-to-all-start.1 = ((f32[16,16,3,128]{3,1,2,0:T(8,128)}), f32[16,16,3,128]{3,1,2,0:T(8,128)S(1)}, u32[]{:S(2)}, u32[]{:S(2)}) async-start(f32[16,16,3,128]{3,1,2,0:T(8,128)} %copy.29), calls=%async_computation.1 | async-start | bytes 786432 | tf_op jit(solution)/shard_map/all_to_all | solution.py:87
  31.1 9.6 %all-to-all-done.1 = f32[16,16,3,128]{3,1,2,0:T(8,128)S(1)} async-done(((f32[16,16,3,128]{3,1,2,0:T(8,128)}), f32[16,16,3,128]{3,1,2,0:T(8,128)S(1)}, u32[]{:S(2)}, u32[]{:S(2)}) %all-to-all-start.1) | async-done | bytes 393248 | tf_op jit(solution)/shard_map/all_to_all | solution.py:87
  40.9 152.2 %while.16 = (s32[]{:T(128)}, f32[65,1025]{1,0:T(8,128)S(1)}, s32[8,4096]{1,0:T(8,128)S(1)}, f32[8,4096]{1,0:T(8,128)S(1)}, f32[8,4096]{1,0:T(8,128)S(1)}, /*index=5*/f32[8,4096]{1,0:T(8,128)S(1)}, s32[]{:T(128)}, s32[]{:T(128)}) while((s32[]{:T(128)}, f32[65,1025]{1,0:T(8,128)S(1)}, s32[8,4096]{1,0:T(8,128)S(1)}, ...), condition=%wide.region_4.5_spmd.clone.clone, body=%wide.region_3.4_spmd.clone.clone.sunk | while | flops 3297597440 | bytes 942707 | solution.py:140
  41.1 18.8 %fusion.98 = f32[65,1025]{1,0:T(8,128)S(1)} fusion(f32[4096]{0:T(1024)S(1)} %bitcast.58, s32[4096]{0:T(1024)S(1)} %get-tuple-element.322, f32[4096]{0:T(1024)S(1)} %broadcast_subtract_fusion.5, s32[4096]{0:T(1024)S(1)} %get-tuple-element.323, f32[4096]{0:T(1024)S(1)} %bitcast.63, f32[4096]{0:T(1024)S(1)} %bitcast.62, s32[4096]{0:T(1024)S(1)} %bitcast.64, ...), kind=kOutput, calls=%fused_computation.15.clone.1 | convolution fusion | flops 3297474560 | bytes 680457 | tf_op jit(solution)/shard_map/while/body/eval_jaxpr/dot_general | solution.py:131
  60.1 18.8 %fusion.98 = f32[65,1025]{1,0:T(8,128)S(1)} fusion(f32[4096]{0:T(1024)S(1)} %bitcast.58, s32[4096]{0:T(1024)S(1)} %get-tuple-element.322, f32[4096]{0:T(1024)S(1)} %broadcast_subtract_fusion.5, s32[4096]{0:T(1024)S(1)} %get-tuple-element.323, f32[4096]{0:T(1024)S(1)} %bitcast.63, f32[4096]{0:T(1024)S(1)} %bitcast.62, s32[4096]{0:T(1024)S(1)} %bitcast.64, ...), kind=kOutput, calls=%fused_computation.15.clone.1 | convolution fusion | flops 3297474560 | bytes 680457 | tf_op jit(solution)/shard_map/while/body/eval_jaxpr/dot_general | solution.py:131
  79.1 18.8 %fusion.98 = f32[65,1025]{1,0:T(8,128)S(1)} fusion(f32[4096]{0:T(1024)S(1)} %bitcast.58, s32[4096]{0:T(1024)S(1)} %get-tuple-element.322, f32[4096]{0:T(1024)S(1)} %broadcast_subtract_fusion.5, s32[4096]{0:T(1024)S(1)} %get-tuple-element.323, f32[4096]{0:T(1024)S(1)} %bitcast.63, f32[4096]{0:T(1024)S(1)} %bitcast.62, s32[4096]{0:T(1024)S(1)} %bitcast.64, ...), kind=kOutput, calls=%fused_computation.15.clone.1 | convolution fusion | flops 3297474560 | bytes 680457 | tf_op jit(solution)/shard_map/while/body/eval_jaxpr/dot_general | solution.py:131
  98.1 18.8 %fusion.98 = f32[65,1025]{1,0:T(8,128)S(1)} fusion(f32[4096]{0:T(1024)S(1)} %bitcast.58, s32[4096]{0:T(1024)S(1)} %get-tuple-element.322, f32[4096]{0:T(1024)S(1)} %broadcast_subtract_fusion.5, s32[4096]{0:T(1024)S(1)} %get-tuple-element.323, f32[4096]{0:T(1024)S(1)} %bitcast.63, f32[4096]{0:T(1024)S(1)} %bitcast.62, s32[4096]{0:T(1024)S(1)} %bitcast.64, ...), kind=kOutput, calls=%fused_computation.15.clone.1 | convolution fusion | flops 3297474560 | bytes 680457 | tf_op jit(solution)/shard_map/while/body/eval_jaxpr/dot_general | solution.py:131
  117.1 18.8 %fusion.98 = f32[65,1025]{1,0:T(8,128)S(1)} fusion(f32[4096]{0:T(1024)S(1)} %bitcast.58, s32[4096]{0:T(1024)S(1)} %get-tuple-element.322, f32[4096]{0:T(1024)S(1)} %broadcast_subtract_fusion.5, s32[4096]{0:T(1024)S(1)} %get-tuple-element.323, f32[4096]{0:T(1024)S(1)} %bitcast.63, f32[4096]{0:T(1024)S(1)} %bitcast.62, s32[4096]{0:T(1024)S(1)} %bitcast.64, ...), kind=kOutput, calls=%fused_computation.15.clone.1 | convolution fusion | flops 3297474560 | bytes 680457 | tf_op jit(solution)/shard_map/while/body/eval_jaxpr/dot_general | solution.py:131
  136.1 18.8 %fusion.98 = f32[65,1025]{1,0:T(8,128)S(1)} fusion(f32[4096]{0:T(1024)S(1)} %bitcast.58, s32[4096]{0:T(1024)S(1)} %get-tuple-element.322, f32[4096]{0:T(1024)S(1)} %broadcast_subtract_fusion.5, s32[4096]{0:T(1024)S(1)} %get-tuple-element.323, f32[4096]{0:T(1024)S(1)} %bitcast.63, f32[4096]{0:T(1024)S(1)} %bitcast.62, s32[4096]{0:T(1024)S(1)} %bitcast.64, ...), kind=kOutput, calls=%fused_computation.15.clone.1 | convolution fusion | flops 3297474560 | bytes 680457 | tf_op jit(solution)/shard_map/while/body/eval_jaxpr/dot_general | solution.py:131
  155.1 18.8 %fusion.98 = f32[65,1025]{1,0:T(8,128)S(1)} fusion(f32[4096]{0:T(1024)S(1)} %bitcast.58, s32[4096]{0:T(1024)S(1)} %get-tuple-element.322, f32[4096]{0:T(1024)S(1)} %broadcast_subtract_fusion.5, s32[4096]{0:T(1024)S(1)} %get-tuple-element.323, f32[4096]{0:T(1024)S(1)} %bitcast.63, f32[4096]{0:T(1024)S(1)} %bitcast.62, s32[4096]{0:T(1024)S(1)} %bitcast.64, ...), kind=kOutput, calls=%fused_computation.15.clone.1 | convolution fusion | flops 3297474560 | bytes 680457 | tf_op jit(solution)/shard_map/while/body/eval_jaxpr/dot_general | solution.py:131
  174.1 18.8 %fusion.98 = f32[65,1025]{1,0:T(8,128)S(1)} fusion(f32[4096]{0:T(1024)S(1)} %bitcast.58, s32[4096]{0:T(1024)S(1)} %get-tuple-element.322, f32[4096]{0:T(1024)S(1)} %broadcast_subtract_fusion.5, s32[4096]{0:T(1024)S(1)} %get-tuple-element.323, f32[4096]{0:T(1024)S(1)} %bitcast.63, f32[4096]{0:T(1024)S(1)} %bitcast.62, s32[4096]{0:T(1024)S(1)} %bitcast.64, ...), kind=kOutput, calls=%fused_computation.15.clone.1 | convolution fusion | flops 3297474560 | bytes 680457 | tf_op jit(solution)/shard_map/while/body/eval_jaxpr/dot_general | solution.py:131
  199.7 3.5 collective-permute-done.1
  204.1 8.9 %reduce-scatter.2.cloned.1.call-done = f32[32,1024]{1,0:T(8,128)} async-done(((f32[64,1024]{1,0:T(8,128)}), f32[32,1024]{1,0:T(8,128)}) %reduce-scatter.2.cloned.1.call-update) | async-done | bytes 131088 | tf_op jit(solution)/shard_map/reduce_scatter | solution.py:150
  226.8 11.2 %all-reduce.4 = (f32[]{:T(128)}, f32[]{:T(128)}) all-reduce(f32[]{:T(128)} %get-tuple-element.194, f32[]{:T(128)} %get-tuple-element.193), channel_id=1, replica_groups=mesh['lat'=4,'lon'=4,'obs'=2] {'lon','obs'}, use_global_device_ids=true, to_apply=%region_8.9 | all-reduce | flops 2 | bytes 16 | tf_op jit(solution)/shard_map/psum | solution.py:10
  238.0 12.3 %all-reduce.9 = (f32[]{:T(128)}, f32[]{:T(128)}) all-reduce(f32[]{:T(128)} %get-tuple-element.215, f32[]{:T(128)} %get-tuple-element.216), channel_id=1, replica_groups=mesh['lat'=4,'lon'=4,'obs'=2] {'lat'}, use_global_device_ids=true, to_apply=%region_9.10 | all-reduce | flops 2 | bytes 16 | tf_op jit(solution)/shard_map/psum | solution.py:11
  258.7 3.2 collective-permute-done.13
  262.9 11.6 %all-reduce.3 = (f32[]{:T(128)}, f32[]{:T(128)}) all-reduce(f32[]{:T(128)} %get-tuple-element.192, f32[]{:T(128)} %get-tuple-element.191), channel_id=1, replica_groups=mesh['lat'=4,'lon'=4,'obs'=2] {'lon','obs'}, use_global_device_ids=true, to_apply=%region_14.15 | all-reduce | flops 2 | bytes 16 | tf_op jit(solution)/shard_map/psum | solution.py:10
  274.5 12.6 %all-reduce.8 = (f32[]{:T(128)}, f32[]{:T(128)}) all-reduce(f32[]{:T(128)} %get-tuple-element.213, f32[]{:T(128)} %get-tuple-element.214), channel_id=1, replica_groups=mesh['lat'=4,'lon'=4,'obs'=2] {'lat'}, use_global_device_ids=true, to_apply=%region_15.16 | all-reduce | flops 2 | bytes 16 | tf_op jit(solution)/shard_map/psum | solution.py:11
  294.9 3.0 collective-permute-start.16
  299.9 2.7 collective-permute-done.17
  303.5 12.6 %all-reduce.2 = (f32[]{:T(128)}, f32[]{:T(128)}) all-reduce(f32[]{:T(128)} %get-tuple-element.190, f32[]{:T(128)} %get-tuple-element.189), channel_id=1, replica_groups=mesh['lat'=4,'lon'=4,'obs'=2] {'lon','obs'}, use_global_device_ids=true, to_apply=%region_20.21 | all-reduce | flops 2 | bytes 16 | tf_op jit(solution)/shard_map/psum | solution.py:10
  316.1 12.6 %all-reduce.7 = (f32[]{:T(128)}, f32[]{:T(128)}) all-reduce(f32[]{:T(128)} %get-tuple-element.211, f32[]{:T(128)} %get-tuple-element.212), channel_id=1, replica_groups=mesh['lat'=4,'lon'=4,'obs'=2] {'lat'}, use_global_device_ids=true, to_apply=%region_21.22 | all-reduce | flops 2 | bytes 16 | tf_op jit(solution)/shard_map/psum | solution.py:11
  335.9 3.0 collective-permute-start.20
  340.8 2.7 collective-permute-done.21
  344.5 12.6 %all-reduce.1 = (f32[]{:T(128)}, f32[]{:T(128)}) all-reduce(f32[]{:T(128)} %get-tuple-element.188, f32[]{:T(128)} %get-tuple-element.187), channel_id=1, replica_groups=mesh['lat'=4,'lon'=4,'obs'=2] {'lon','obs'}, use_global_device_ids=true, to_apply=%region_26.27 | all-reduce | flops 2 | bytes 16 | tf_op jit(solution)/shard_map/psum | solution.py:10
  357.1 12.6 %all-reduce.6 = (f32[]{:T(128)}, f32[]{:T(128)}) all-reduce(f32[]{:T(128)} %get-tuple-element.209, f32[]{:T(128)} %get-tuple-element.210), channel_id=1, replica_groups=mesh['lat'=4,'lon'=4,'obs'=2] {'lat'}, use_global_device_ids=true, to_apply=%region_27.28 | all-reduce | flops 2 | bytes 16 | tf_op jit(solution)/shard_map/psum | solution.py:11
  376.9 3.0 collective-permute-start.24
  381.9 2.7 collective-permute-done.25
  385.5 12.6 %all-reduce = (f32[]{:T(128)}, f32[]{:T(128)}) all-reduce(f32[]{:T(128)} %get-tuple-element.186, f32[]{:T(128)} %get-tuple-element.185), channel_id=1, replica_groups=mesh['lat'=4,'lon'=4,'obs'=2] {'lon','obs'}, use_global_device_ids=true, to_apply=%region_32.33 | all-reduce | flops 2 | bytes 16 | tf_op jit(solution)/shard_map/psum | solution.py:10
  398.1 12.6 %all-reduce.5 = (f32[]{:T(128)}, f32[]{:T(128)}) all-reduce(f32[]{:T(128)} %get-tuple-element.207, f32[]{:T(128)} %get-tuple-element.208), channel_id=1, replica_groups=mesh['lat'=4,'lon'=4,'obs'=2] {'lat'}, use_global_device_ids=true, to_apply=%region_33.34 | all-reduce | flops 2 | bytes 16 | tf_op jit(solution)/shard_map/psum | solution.py:11
  (154 shorter events, 54.4 us)
Async XLA Ops:
  11.3 12.7 %all-to-all-start = ((s32[16,16,128]{2,1,0:T(8,128)}), s32[16,16,128]{2,1,0:T(8,128)S(1)}, u32[]{:S(2)}, u32[]{:S(2)}) async-start(s32[16,16,128]{2,1,0:T(8,128)} %bitcast.5), calls=%async_computation | async-start | bytes 262144 | tf_op jit(solution)/shard_map/all_to_all | solution.py:94
  24.0 16.7 %all-to-all-start.1 = ((f32[16,16,3,128]{3,1,2,0:T(8,128)}), f32[16,16,3,128]{3,1,2,0:T(8,128)S(1)}, u32[]{:S(2)}, u32[]{:S(2)}) async-start(f32[16,16,3,128]{3,1,2,0:T(8,128)} %copy.29), calls=%async_computation.1 | async-start | bytes 786432 | tf_op jit(solution)/shard_map/all_to_all | solution.py:87
  31.0 182.0 %reduce-scatter.2.cloned.1.call-start = ((), (), s32[]{:S(2)}) async-start(), calls=%async_computation.3 | async-start | bytes 393216 | tf_op jit(solution)/shard_map/reduce_scatter | solution.py:150
  193.2 3.6 collective-permute-start
  196.2 16.8 %copy-start.2 = (f32[32,1024]{1,0:T(8,128)S(1)}, f32[32,1024]{1,0:T(8,128)}, u32[]{:S(2)}) copy-start(f32[32,1024]{1,0:T(8,128)} %param.23) | copy-start | bytes 393220
  196.2 16.8 %copy-start.3 = (s32[32,1024]{1,0:T(8,128)S(1)}, s32[32,1024]{1,0:T(8,128)}, u32[]{:S(2)}) copy-start(s32[32,1024]{1,0:T(8,128)} %param.21) | copy-start | bytes 393220
  197.8 5.5 %collective-permute-start.1 = (f32[1024]{0:T(1024)S(1)}, f32[1024]{0:T(1024)S(1)}, u32[]{:S(2)}, u32[]{:S(2)}) collective-permute-start(f32[1024]{0:T(1024)S(1)} %bitcast.68), channel_id=1, source_target_pairs={{0,8},{8,16},{16,24},{1,9},{9,17},{17,25},{2,10},{10,18},{18,26},{... | collective-permute-start | bytes 12296 | tf_op jit(solution)/shard_map/ppermute | solution.py:37
  204.1 21.8 %copy-start = (f32[32,1024]{1,0:T(8,128)S(1)}, f32[32,1024]{1,0:T(8,128)}, u32[]{:S(2)}) copy-start(f32[32,1024]{1,0:T(8,128)} %param.22) | copy-start | bytes 393220
  214.0 3.6 collective-permute-start.2
  214.4 3.2 collective-permute-start.3
  215.8 3.9 collective-permute-start.6
  215.8 3.9 collective-permute-start.7
  217.7 4.1 collective-permute-start.4
  218.2 4.8 %collective-permute-start.5 = (f32[34,1]{1,0:T(8,128)S(1)}, f32[34,1]{1,0:T(8,128)S(1)}, u32[]{:S(2)}, u32[]{:S(2)}) collective-permute-start(f32[34,1]{1,0:T(8,128)S(1)} %get-tuple-element.254), channel_id=1, source_target_pairs={{2,0},{4,2},{6,4},{0,6},{3,1},{5,3},{7,5},{1,7},{10,8},{12,10},{14... | collective-permute-start | bytes 416 | tf_op jit(solution)/shard_map/ppermute | solution.py:23
  219.8 3.8 collective-permute-start.8
  221.2 4.7 %collective-permute-start.9 = (f32[34,1]{1,0:T(8,128)S(1)}, f32[34,1]{1,0:T(8,128)S(1)}, u32[]{:S(2)}, u32[]{:S(2)}) collective-permute-start(f32[34,1]{1,0:T(8,128)S(1)} %get-tuple-element.256), channel_id=1, source_target_pairs={{2,0},{4,2},{6,4},{0,6},{3,1},{5,3},{7,5},{1,7},{10,8},{12,10},{14... | collective-permute-start | bytes 416 | tf_op jit(solution)/shard_map/ppermute | solution.py:23
  251.7 3.1 collective-permute-start.10
  251.8 3.1 collective-permute-start.11
  254.9 3.8 collective-permute-start.12
  257.1 4.8 %collective-permute-start.13 = (f32[34,1]{1,0:T(8,128)S(1)}, f32[34,1]{1,0:T(8,128)S(1)}, u32[]{:S(2)}, u32[]{:S(2)}) collective-permute-start(f32[34,1]{1,0:T(8,128)S(1)} %get-tuple-element.252), channel_id=1, source_target_pairs={{2,0},{4,2},{6,4},{0,6},{3,1},{5,3},{7,5},{1,7},{10,8},{12,10},{14... | collective-permute-start | bytes 416 | tf_op jit(solution)/shard_map/ppermute | solution.py:23
  291.7 3.1 collective-permute-start.14
  291.8 3.1 collective-permute-start.15
  294.9 4.9 %collective-permute-start.16 = (f32[34,1]{1,0:T(8,128)S(1)}, f32[34,1]{1,0:T(8,128)S(1)}, u32[]{:S(2)}, u32[]{:S(2)}) collective-permute-start(f32[34,1]{1,0:T(8,128)S(1)} %get-tuple-element.249), channel_id=1, source_target_pairs={{0,2},{2,4},{4,6},{6,0},{1,3},{3,5},{5,7},{7,1},{8,10},{10,12},{12... | collective-permute-start | bytes 416 | tf_op jit(solution)/shard_map/ppermute | solution.py:20
  297.9 4.7 %collective-permute-start.17 = (f32[34,1]{1,0:T(8,128)S(1)}, f32[34,1]{1,0:T(8,128)S(1)}, u32[]{:S(2)}, u32[]{:S(2)}) collective-permute-start(f32[34,1]{1,0:T(8,128)S(1)} %get-tuple-element.250), channel_id=1, source_target_pairs={{2,0},{4,2},{6,4},{0,6},{3,1},{5,3},{7,5},{1,7},{10,8},{12,10},{14... | collective-permute-start | bytes 416 | tf_op jit(solution)/shard_map/ppermute | solution.py:23
  332.7 3.1 collective-permute-start.18
  332.8 3.1 collective-permute-start.19
  335.9 4.9 %collective-permute-start.20 = (f32[34,1]{1,0:T(8,128)S(1)}, f32[34,1]{1,0:T(8,128)S(1)}, u32[]{:S(2)}, u32[]{:S(2)}) collective-permute-start(f32[34,1]{1,0:T(8,128)S(1)} %get-tuple-element.247), channel_id=1, source_target_pairs={{0,2},{2,4},{4,6},{6,0},{1,3},{3,5},{5,7},{7,1},{8,10},{10,12},{12... | collective-permute-start | bytes 416 | tf_op jit(solution)/shard_map/ppermute | solution.py:20
  338.9 4.7 %collective-permute-start.21 = (f32[34,1]{1,0:T(8,128)S(1)}, f32[34,1]{1,0:T(8,128)S(1)}, u32[]{:S(2)}, u32[]{:S(2)}) collective-permute-start(f32[34,1]{1,0:T(8,128)S(1)} %get-tuple-element.248), channel_id=1, source_target_pairs={{2,0},{4,2},{6,4},{0,6},{3,1},{5,3},{7,5},{1,7},{10,8},{12,10},{14... | collective-permute-start | bytes 416 | tf_op jit(solution)/shard_map/ppermute | solution.py:23
  373.7 3.1 collective-permute-start.22
  373.8 3.1 collective-permute-start.23
  376.9 4.9 %collective-permute-start.24 = (f32[34,1]{1,0:T(8,128)S(1)}, f32[34,1]{1,0:T(8,128)S(1)}, u32[]{:S(2)}, u32[]{:S(2)}) collective-permute-start(f32[34,1]{1,0:T(8,128)S(1)} %get-tuple-element.245), channel_id=1, source_target_pairs={{0,2},{2,4},{4,6},{6,0},{1,3},{3,5},{5,7},{7,1},{8,10},{10,12},{12... | collective-permute-start | bytes 416 | tf_op jit(solution)/shard_map/ppermute | solution.py:20
  379.9 4.7 %collective-permute-start.25 = (f32[34,1]{1,0:T(8,128)S(1)}, f32[34,1]{1,0:T(8,128)S(1)}, u32[]{:S(2)}, u32[]{:S(2)}) collective-permute-start(f32[34,1]{1,0:T(8,128)S(1)} %get-tuple-element.246), channel_id=1, source_target_pairs={{2,0},{4,2},{6,4},{0,6},{3,1},{5,3},{7,5},{1,7},{10,8},{12,10},{14... | collective-permute-start | bytes 416 | tf_op jit(solution)/shard_map/ppermute | solution.py:23
  (4 other events, 34.6 us)
Sparse Core Ops, SparseCore 0:
  204.2 8.7 reduce-scatter.1
